TPU v7x, 32 devices: a whole 2x2x4 slice. The times are simulated.
32 devices in a mesh: seq: 2 (over core), heads: 4 (over y, x), batch: 4 (over z).
Axes of the slice: x: 2, y: 2, z: 4, core: 2. Of those that a mesh axis runs over, the one named last changes fastest.
Arguments:
- queries: bfloat16 [4, 512, 8192], P('batch', 'seq', 'heads'), may hold values from -160 to 160
- keys: bfloat16 [4, 512, 1024], P('batch', 'seq', 'heads'), may hold values from -7 to 7
- values: bfloat16 [4, 512, 1024], P('batch', 'seq', 'heads'), may hold values from -6 to 6
- doc_lengths: int32 [4, 16], P('batch'), may hold values from 1 to 384, 512 in all within a row
- out_weight: bfloat16 [8192, 8192], P('heads', 'batch'), may hold values from -0.0625 to 0.0625
Outputs:
- projected: bfloat16 [4, 512, 8192], P('heads', 'seq', 'batch')
Inputs may be any that keep to these rules, and one draw needn't show every extreme that they name: `doc_lengths`: each row sums to 512; no document is longer than 384 tokens and one is exactly 384.
All inputs are finite; a program needn't handle non-finite values.
Results may differ from a plain program's by a relative error of at most 0.012.
Values may be sent and summed in bfloat16 or wider, within the bound.
A program may use at most 64 MiB of HBM per device.

v0:
```python
import jax
import jax.numpy as jnp
from jax import lax
from jax.sharding import PartitionSpec as P

HEAD_WIDTH = 128
DOCS = 16


def shifted(x, axis, by):
    peers = lax.axis_size(axis)
    pairs = [(i, i + by) for i in range(peers) if 0 <= i + by < peers]
    return lax.ppermute(x, axis, pairs)


def per_device(queries, keys, values, doc_lengths, out_weight):
    shard_len = queries.shape[1]
    q_width = queries.shape[2]
    kv_width = keys.shape[2]
    kv_heads = kv_width // HEAD_WIDTH
    q_groups = q_width // kv_width
    seq_total = lax.axis_size("seq") * shard_len
    shard_start = lax.axis_index("seq") * shard_len
    doc_ends = jnp.cumsum(doc_lengths[0])
    doc_starts = doc_ends - doc_lengths[0]
    all_positions = jnp.arange(seq_total, dtype=jnp.int32)
    doc_of = jnp.sum((all_positions[:, None] >= doc_ends[None, :]).astype(jnp.int32), axis=1)
    query_pos = shard_start + jnp.arange(shard_len, dtype=jnp.int32)
    query_doc = lax.dynamic_slice_in_dim(doc_of, shard_start, shard_len, 0)
    reach_start = jnp.sum(
        jnp.where(jnp.arange(DOCS, dtype=jnp.int32) == query_doc[0], doc_starts, 0)
    )
    query_heads = queries[0].reshape(shard_len, kv_heads, q_groups, HEAD_WIDTH)
    factor = HEAD_WIDTH ** (-0.5)

    def absorb(carried, key_block, value_block, key_start):
        key_count = key_block.shape[0]

        def attend(current):
            running, totals, weighted = current
            key_heads = key_block.reshape(key_count, kv_heads, HEAD_WIDTH)
            value_heads = value_block.reshape(key_count, kv_heads, HEAD_WIDTH)
            scores = (
                jnp.einsum(
                    "qhgd,khd->hgqk", query_heads, key_heads, preferred_element_type=jnp.float32
                )
                * factor
            )
            key_pos = key_start + jnp.arange(key_count, dtype=jnp.int32)
            key_doc = lax.dynamic_slice_in_dim(doc_of, key_start, key_count, 0)
            allowed = (query_doc[:, None] == key_doc[None, :]) & (
                key_pos[None, :] <= query_pos[:, None]
            )
            scores = jnp.where(allowed, scores, -jnp.inf)
            raised = jnp.maximum(running, jnp.max(scores, axis=-1))
            shrink = jnp.exp(running - raised)
            weights = jnp.exp(scores - raised[..., None])
            totals = totals * shrink + jnp.sum(weights, axis=-1)
            summed = jnp.einsum(
                "hgqk,khd->qhgd",
                weights.astype(jnp.bfloat16),
                value_heads,
                preferred_element_type=jnp.float32,
            )
            weighted = weighted * jnp.transpose(shrink, (2, 0, 1))[..., None] + summed
            return (raised, totals, weighted)

        needed = (
            (key_start >= 0)
            & (key_start + key_count > reach_start)
            & (key_start < shard_start + shard_len)
        )
        return lax.cond(needed, attend, lambda current: current, carried)

    initial = (
        jnp.full((kv_heads, q_groups, shard_len), -1e30, jnp.float32),
        jnp.zeros((kv_heads, q_groups, shard_len), jnp.float32),
        jnp.zeros((shard_len, kv_heads, q_groups, HEAD_WIDTH), jnp.float32),
    )
    longest = seq_total // 2 + shard_len // 2
    reach_back = min((longest + shard_len - 2) // shard_len, lax.axis_size("seq") - 1)
    finished = absorb(initial, keys[0], values[0], shard_start)
    stacked = jnp.stack((keys[0], values[0]))
    for distance in range(1, reach_back + 1):
        earlier = shifted(stacked, "seq", distance)
        finished = absorb(finished, earlier[0], earlier[1], shard_start - distance * shard_len)
    running, totals, weighted = finished
    attended = (weighted / jnp.transpose(totals, (2, 0, 1))[..., None]).astype(jnp.bfloat16)
    attended = attended.reshape(1, shard_len, q_width)
    gathered = lax.all_gather(attended, "batch", axis=0, tiled=True)
    flat_rows = gathered.reshape(-1, q_width)
    owned_rows = lax.psum_scatter(
        jnp.dot(flat_rows, out_weight, preferred_element_type=jnp.float32).astype(jnp.bfloat16),
        "heads",
        scatter_dimension=0,
        tiled=True,
    )
    return owned_rows.reshape(-1, shard_len, out_weight.shape[1])


def solution(mesh):
    return jax.shard_map(
        per_device,
        mesh=mesh,
        in_specs=(
            P("batch", "seq", "heads"),
            P("batch", "seq", "heads"),
            P("batch", "seq", "heads"),
            P("batch", None),
            P("heads", "batch"),
        ),
        out_specs=P("heads", "seq", "batch"),
        check_vma=False,
    )
```

profile of v0, /device:TPU:24, one launch (start us, length us, event | category | flops | bytes accessed | tf_op | source)
XLA Modules:
  0.0 190.2 jit_solution(8676593514843635642)
XLA Ops:
  6.5 1.0 copy.61
  7.5 1.0 copy.62
  8.6 0.7 pad_maximum_fusion
  9.3 1.7 collective-permute-start
  11.0 0.7 copy.58
  11.8 0.1 reduce
  11.9 0.1 convert_reduce_fusion
  12.0 0.1 dynamic_slice.9
  12.1 0.6 slice.11
  12.7 2.0 %fusion.32 = s32[]{:T(128)} fusion(s32[16]{0:T(128)S(1)} %reduce, s32[1,16]{1,0:T(1,128)} %param.12, s32[]{:T(128)} %bitcast.13), kind=kLoop, calls=%fused_computation.47 | loop fusion | flops 63 | bytes 136 | tf_op jit(solution)/shard_map/reduce_sum | solution.py:30
  15.8 1.5 copy.59
  17.3 8.7 %conditional.2 = (f32[2,8,256]{2,1,0:T(8,128)}, f32[2,8,256]{2,1,0:T(8,128)S(1)}, f32[256,2,8,128]{3,0,2,1:T(8,128)S(1)}) conditional(s32[]{:T(128)} %convert_element_type.23, () %tuple.20, (s32[256]{0:T(256)S(1)}, s32[]{:T(128)}, s32[512]{0:T(512)S(1)}, s32[256]{0:T(256)S(1)}, bf16[1,256,256]{2,1,0:T(8,128)(2,1)}, ...), branch_computations={%region_3.4_spmd, %region_4.7_spmd} | conditional | flops 549142784 | bytes 17488990 | solution.py:73
  17.3 0.1 dynamic_slice.6
  17.4 0.1 compare_and_fusion
  17.6 1.6 reshape_squeeze.11
  19.1 0.9 reshape_squeeze.10
  20.1 0.8 fusion.2
  20.9 0.6 fusion.14
  21.5 1.6 fusion.1
  23.0 2.3 %bitcast_add_fusion = f32[256,2,8,128]{3,0,2,1:T(8,128)S(1)} fusion(f32[2,256,256,8]{2,1,3,0:T(8,128)S(1)} %get-tuple-element.146, f32[2,8,256]{2,1,0:T(8,128)} %get-tuple-element.150, pred[256,256]{0,1:T(8,128)(4,1)S(1)} %compare_and_fusion, f32[256,2,8]{0,2,1:T(8,128)S(1)} %get-tuple-element.137, bf16[256,2,128,1]{2,1,0,3:T(2,128)(2,1)S(1)} %bitcast.66), kind=kOutput, calls=%fused_computation.6 | convolution fusion | flops 273154048 | bytes 6520832 | tf_op jit(solution)/shard_map/cond/branch_1_fun/hgqk,khd->qhgd/dot_general | solution.py:59
  25.3 0.7 fusion.15
  26.0 0.0 collective-permute-done
  26.1 1.9 conditional.3
  26.1 1.9 copy.82
  28.0 1.8 divide_convert_fusion
  29.8 1.4 copy.65
  31.2 0.0 all-gather.2.cloned.1.call-update
  31.2 0.0 reduce-scatter.2.cloned.1.call-start
  31.3 84.3 %all-gather.2.cloned.1.call-done = bf16[4,256,2048]{2,1,0:T(8,128)(2,1)} async-done(((bf16[1,256,2048]{2,1,0:T(8,128)(2,1)}), bf16[4,256,2048]{2,1,0:T(8,128)(2,1)}) %all-gather.2.cloned.1.call-update) | async-done | bytes 4194320 | tf_op jit(solution)/shard_map/all_gather | solution.py:90
  115.5 13.8 %convolution_convert_fusion = bf16[1024,2048]{1,0:T(8,128)(2,1)} fusion(bf16[1024,2048]{1,0:T(8,128)(2,1)} %bitcast.68, bf16[2048,2048]{1,0:T(8,128)(2,1)} %param.13), kind=kOutput, calls=%fused_computation.40 | convolution fusion | flops 8592031744 | bytes 16777216 | tf_op jit(solution)/shard_map/dot_general | solution.py:93
  129.3 0.0 reduce-scatter.2.cloned.1.call-update
  129.4 54.0 %reduce-scatter.2.cloned.1.call-done = bf16[256,2048]{1,0:T(8,128)(2,1)} async-done(((bf16[1024,2048]{1,0:T(8,128)(2,1)}), bf16[256,2048]{1,0:T(8,128)(2,1)}) %reduce-scatter.2.cloned.1.call-update) | async-done | bytes 1048592 | tf_op jit(solution)/shard_map/reduce_scatter | solution.py:92
  (6 shorter events, 0.0 us)
Async XLA Ops:
  6.5 109.0 %all-gather.2.cloned.1.call-start = ((), (), s32[]{:S(2)}) async-start(), calls=%async_computation.1 | async-start | bytes 5242880 | tf_op jit(solution)/shard_map/all_gather | solution.py:90
  9.3 16.8 %collective-permute-start = (bf16[2,256,256]{1,2,0:T(8,128)(2,1)}, bf16[2,256,256]{1,2,0:T(8,128)(2,1)S(1)}, u32[]{:S(2)}, u32[]{:S(2)}) collective-permute-start(bf16[2,256,256]{1,2,0:T(8,128)(2,1)} %pad_maximum_fusion), channel_id=1, source_target_pairs={{0,16},{1,17},{2,18},{3,19},{4,20},{5,21},{6,22},{7,23},{8,24},{9,... | collective-permute-start | bytes 786440 | tf_op jit(solution)/shard_map/ppermute | solution.py:13
  20.1 3.0 %copy-start.1 = (bf16[256,2,128]{2,1,0:T(2,128)(2,1)S(1)}, bf16[256,2,128]{2,1,0:T(2,128)(2,1)}, u32[]{:S(2)}) copy-start(bf16[256,2,128]{2,1,0:T(2,128)(2,1)} %reshape_squeeze.11) | copy-start | bytes 393220 | tf_op jit(solution)/shard_map/cond
  31.2 152.1 %reduce-scatter.2.cloned.1.call-start = ((), (), s32[]{:S(2)}) async-start(), calls=%async_computation.2 | async-start | bytes 5242880 | tf_op jit(solution)/shard_map/reduce_scatter | solution.py:92
Sparse Core Ops, SparseCore 0:
  31.3 84.1 all-gather.1
  129.5 53.8 reduce-scatter.1
where the time goes:
time: 193 us; the launch traced here: 190 us
  waiting for transfers between devices  138 us (72%)
  matrix products  16.9 us (9%)
  between operations  14.6 us (8%)
  local copies, waits for them, and re-layouts  10.8 us (6%)
  other arithmetic  7.8 us (4%)
    all_gather x1, waiting for transfers between devices, per_device(): gathered = lax.all_gather(attended, 'batch', axis=0, tiled=True)  84.3 us
    reduce_scatter x1, waiting for transfers between devices, per_device(): lax.psum_scatter(jnp.dot(flat_rows, out_weight, preferred_element_type=jn...  54 us
    dot_general x1, matrix products, per_device(): jnp.dot(flat_rows, out_weight, preferred_element_type=jnp.float32)  13.8 us
  transfers between devices with their start and end apart: 3, of which 2 were waited for; matrix products, arithmetic and copies ran while one was open for 7% of the time, Pallas kernels for 0%

commit v1 on v0

v1 whole, which is shorter than its diff:
```python
import functools

import jax
import jax.numpy as jnp
from jax import lax
from jax.experimental import pallas as pl
from jax.experimental.pallas import tpu as pltpu
from jax.sharding import PartitionSpec as P

HEAD_WIDTH = 128
DOCS = 16
PIECES = 4
LAG = 2
STACK = 4
COLS = 512
MESH = pl.DeviceIdType.MESH


def kernel(
    sizes, q_ref, k_ref, v_ref, len_ref, w_hbm, out_ref,
    w_ref, keys, vals, gath, stage, incoming,
    w_sem, kv_send, kv_recv, z_send, z_recv, c_send, c_recv,
):
    seqs, groups, n, reach = sizes
    shard_len, q_width = q_ref.shape[1], q_ref.shape[2]
    kv_heads = k_ref.shape[2] // HEAD_WIDTH
    per_kv = q_width // k_ref.shape[2]
    rows = shard_len // PIECES
    slots = n * PIECES
    half = w_ref.shape[1] // 2
    key_count = keys.shape[0]

    me = lax.axis_index("seq")
    head = lax.axis_index("heads")
    b = lax.axis_index("batch")

    def ring(h):
        return h + h // 2 - 2 * (h // 3) if groups == 4 else h

    place = ring(head)
    ahead = ring(lax.rem(place + 1, groups))
    behind = ring(lax.rem(place + groups - 1, groups))

    w_copy = pltpu.make_async_copy(w_hbm, w_ref, w_sem)
    w_copy.start()

    barrier = pltpu.get_barrier_semaphore()

    def greet(axis, index):
        pl.semaphore_signal(barrier, inc=1, device_id={axis: index}, device_id_type=MESH)

    greet("heads", ahead)
    greet("heads", behind)
    expected = 2
    for cond, index in ((b > 0, b - 1), (b < n - 1, b + 1)):
        expected = expected + cond.astype(jnp.int32)
        pl.when(cond)(functools.partial(greet, "batch", index))
    for d in range(1, reach + 1):
        for cond, index in ((me >= d, me - d), (me + d < seqs, me + d)):
            expected = expected + cond.astype(jnp.int32)
            pl.when(cond)(functools.partial(greet, "seq", index))
    pl.semaphore_wait(barrier, expected)

    def kv_copies(d, target):
        spot = pl.ds((reach - d) * shard_len, shard_len)
        return [
            pltpu.make_async_remote_copy(
                src_ref=src.at[0], dst_ref=dst.at[spot],
                send_sem=kv_send.at[i, d - 1], recv_sem=kv_recv.at[i, d - 1],
                device_id={"seq": target}, device_id_type=MESH,
            )
            for i, (src, dst) in enumerate(((k_ref, keys), (v_ref, vals)))
        ]

    for d in range(1, reach + 1):
        @pl.when(me + d < seqs)
        def _():
            for copy in kv_copies(d, me + d):
                copy.start()

    keys[pl.ds(reach * shard_len, shard_len), :] = k_ref[0]
    vals[pl.ds(reach * shard_len, shard_len), :] = v_ref[0]
    for d in range(1, reach + 1):
        @pl.when(me < d)
        def _():
            spot = pl.ds((reach - d) * shard_len, shard_len)
            keys[spot, :] = jnp.zeros((shard_len, keys.shape[1]), keys.dtype)
            vals[spot, :] = jnp.zeros((shard_len, vals.shape[1]), vals.dtype)

    for d in range(1, reach + 1):
        @pl.when(me >= d)
        def _():
            for copy in kv_copies(d, me - d):
                copy.wait_recv()

    def z_copy(way, source, piece):
        spot = pl.ds(pl.multiple_of(piece * rows, rows), rows)
        return pltpu.make_async_remote_copy(
            src_ref=gath.at[source, spot], dst_ref=gath.at[source, spot],
            send_sem=z_send.at[way, source, piece], recv_sem=z_recv.at[source, piece],
            device_id={"batch": b + 1 if way == 0 else b - 1}, device_id_type=MESH,
        )

    def goes(way, source):
        if way == 0:
            return (source <= b) & (b < n - 1)
        return (source >= b) & (b > 0)

    def pass_on(source, piece):
        for way in range(2):
            @pl.when(goes(way, source))
            def _():
                z_copy(way, source, piece).start()

    factor = HEAD_WIDTH ** (-0.5)
    shard_start = me * shard_len
    first_key = shard_start - reach * shard_len

    def attend(piece, _):
        base = pl.multiple_of(piece * rows, rows)
        row_pos = shard_start + base + lax.broadcasted_iota(jnp.int32, (rows, HEAD_WIDTH), 0)
        start = jnp.zeros((rows, HEAD_WIDTH), jnp.int32)
        end = jnp.int32(0)
        for d in range(DOCS):
            end = end + len_ref[0, d]
            start = jnp.where(row_pos >= end, end, start)
        key_pos = first_key + lax.broadcasted_iota(jnp.int32, (rows, key_count), 1)
        allowed = (key_pos >= start[:, :1]) & (key_pos <= row_pos[:, :1])
        bias = jnp.where(allowed, 0.0, -jnp.inf).astype(jnp.float32)
        bias = jnp.concatenate([bias] * STACK, axis=0)
        for first in range(0, kv_heads * per_kv, STACK):
            g = first // per_kv
            gcols = slice(g * HEAD_WIDTH, (g + 1) * HEAD_WIDTH)
            q = jnp.concatenate(
                [
                    q_ref[0, pl.ds(base, rows), j * HEAD_WIDTH:(j + 1) * HEAD_WIDTH]
                    for j in range(first, first + STACK)
                ],
                axis=0,
            )
            scores = lax.dot_general(
                q, keys[:, gcols], (((1,), (1,)), ((), ())),
                preferred_element_type=jnp.float32,
            ) * factor + bias
            weights = jnp.exp(scores - jnp.max(scores, axis=1, keepdims=True))
            total = jnp.sum(weights, axis=1, keepdims=True)
            summed = jnp.dot(
                weights.astype(jnp.bfloat16), vals[:, gcols],
                preferred_element_type=jnp.float32,
            )
            result = (summed / total).astype(jnp.bfloat16)
            for i in range(STACK):
                j = first + i
                gath[b, pl.ds(base, rows), j * HEAD_WIDTH:(j + 1) * HEAD_WIDTH] = (
                    result[i * rows:(i + 1) * rows]
                )
        pass_on(b, piece)
        return 0

    lax.fori_loop(0, PIECES, attend, 0)
    w_copy.wait()

    both = jnp.minimum(b, n - 1 - b)

    def slot_of(slot):
        u = jnp.maximum(slot - PIECES, 0)
        v = jnp.maximum(slot - PIECES - 2 * PIECES * both, 0)
        near_d = u // (2 * PIECES) + 1
        near_v = lax.rem(u, 2 * PIECES)
        near_seq = jnp.where(lax.rem(near_v, 2) == 0, b - near_d, b + near_d)
        far_d = both + 1 + v // PIECES
        far_seq = jnp.where(b > n - 1 - b, b - far_d, b + far_d)
        is_own = slot < PIECES
        is_near = slot < PIECES + 2 * PIECES * both
        seq = jnp.where(is_own, b, jnp.where(is_near, near_seq, far_seq))
        piece = jnp.where(is_own, slot, jnp.where(is_near, near_v // 2, lax.rem(v, PIECES)))
        return seq, piece

    def steps_from_root(way, source):
        gap = place - ring(source) if way == 0 else ring(source) - place
        return lax.rem(gap + groups, groups)

    def chain_copy(way, source, piece):
        return pltpu.make_async_remote_copy(
            src_ref=stage.at[way, source, piece], dst_ref=incoming.at[way, source, piece],
            send_sem=c_send.at[way, source, piece], recv_sem=c_recv.at[way, source, piece],
            device_id={"heads": ahead if way == 0 else behind}, device_id_type=MESH,
        )

    def hop(h, slot):
        source, piece = slot_of(slot)
        for way in range(2):
            @pl.when(steps_from_root(way, source) == (h + 1) % groups)
            def _():
                chain_copy(way, source, piece).wait_recv()
                merged = (
                    incoming[way, source, piece].astype(jnp.float32)
                    + stage[way, source, piece].astype(jnp.float32)
                ).astype(jnp.bfloat16)
                if h < groups - 1:
                    stage[way, source, piece] = merged
                    chain_copy(way, source, piece).start()
                else:
                    spot = pl.ds(pl.multiple_of(piece * rows, rows), rows)
                    out_ref[0, spot, way * half:(way + 1) * half] = merged

    def step(i, _):
        @pl.when(i < slots)
        def _():
            source, piece = slot_of(i)

            @pl.when(source != b)
            def _():
                z_copy(0, source, piece).wait_recv()
                pass_on(source, piece)

            spot = pl.ds(pl.multiple_of(piece * rows, rows), rows)
            for way in range(2):
                def tile(t, _):
                    cols = pl.multiple_of(t * COLS, COLS)
                    stage[way, source, piece, :, pl.ds(cols, COLS)] = jnp.dot(
                        gath[source, spot, :],
                        w_ref[:, pl.ds(pl.multiple_of(way * half + cols, COLS), COLS)],
                        preferred_element_type=jnp.float32,
                    ).astype(jnp.bfloat16)
                    return 0

                lax.fori_loop(0, half // COLS, tile, 0)

                @pl.when(steps_from_root(way, source) == 1)
                def _():
                    chain_copy(way, source, piece).start()

        for h in range(1, groups):
            slot = i - h * LAG

            @pl.when((slot >= 0) & (slot < slots))
            def _():
                hop(h, slot)

        return 0

    lax.fori_loop(0, slots + (groups - 1) * LAG, step, 0)

    for d in range(1, reach + 1):
        @pl.when(me + d < seqs)
        def _():
            for copy in kv_copies(d, me + d):
                copy.wait_send()

    def finish(slot, _):
        source, piece = slot // PIECES, lax.rem(slot, PIECES)
        for way in range(2):
            @pl.when(goes(way, source))
            def _():
                z_copy(way, source, piece).wait_send()

            @pl.when(steps_from_root(way, source) != 0)
            def _():
                chain_copy(way, source, piece).wait_send()

        return 0

    lax.fori_loop(0, slots, finish, 0)


def solution(mesh):
    seqs, groups, n = mesh.shape["seq"], mesh.shape["heads"], mesh.shape["batch"]

    def per_device(queries, keys, values, doc_lengths, out_weight):
        shard_len, q_width = queries.shape[1:]
        kv_width = keys.shape[2]
        columns = out_weight.shape[1]
        seq_total = seqs * shard_len
        longest = seq_total // 2 + shard_len // 2
        reach = min((longest + shard_len - 2) // shard_len, seqs - 1)
        rows = shard_len // PIECES
        key_count = (reach + 1) * shard_len
        vmem = pl.BlockSpec(memory_space=pltpu.VMEM)
        dma = pltpu.SemaphoreType.DMA
        return pl.pallas_call(
            functools.partial(kernel, (seqs, groups, n, reach)),
            out_shape=jax.ShapeDtypeStruct((1, shard_len, columns), jnp.bfloat16),
            in_specs=[
                vmem, vmem, vmem,
                pl.BlockSpec(memory_space=pltpu.SMEM),
                pl.BlockSpec(memory_space=pl.ANY),
            ],
            out_specs=vmem,
            scratch_shapes=[
                pltpu.VMEM(out_weight.shape, jnp.bfloat16),
                pltpu.VMEM((key_count, kv_width), jnp.bfloat16),
                pltpu.VMEM((key_count, kv_width), jnp.bfloat16),
                pltpu.VMEM((n, shard_len, q_width), jnp.bfloat16),
                pltpu.VMEM((2, n, PIECES, rows, columns // 2), jnp.bfloat16),
                pltpu.VMEM((2, n, PIECES, rows, columns // 2), jnp.bfloat16),
                dma,
                dma((2, max(reach, 1))),
                dma((2, max(reach, 1))),
                dma((2, n, PIECES)),
                dma((n, PIECES)),
                dma((2, n, PIECES)),
                dma((2, n, PIECES)),
            ],
            compiler_params=pltpu.CompilerParams(
                collective_id=0, has_side_effects=True, vmem_limit_bytes=60 * 2**20
            ),
        )(queries, keys, values, doc_lengths, out_weight)

    return jax.shard_map(
        per_device,
        mesh=mesh,
        in_specs=(
            P("batch", "seq", "heads"),
            P("batch", "seq", "heads"),
            P("batch", "seq", "heads"),
            P("batch", None),
            P("heads", "batch"),
        ),
        out_specs=P("heads", "seq", "batch"),
        check_vma=False,
    )
```

time: 193 us -> 99.7 us (0.52); the launches traced: 190 us -> 99.6 us
  waiting for transfers between devices: 138 us -> 0 us
  Pallas kernels: 0 us -> 97.2 us
  matrix products: 16.9 us -> 0 us
  between operations: 14.6 us -> 0.01 us
  local copies, waits for them, and re-layouts: 10.8 us -> 2.3 us
  other arithmetic: 7.8 us -> 0 us
    pallas_call x0 -> x1, Pallas kernels: none -> 97.2 us  [per_device(): pl.pallas_call(functools.partial(kernel, (seqs, groups, n, reach)), out_s...]
    all_gather x1 -> x0, waiting for transfers between devices: 84.3 us -> none  [per_device(): gathered = lax.all_gather(attended, 'batch', axis=0, tiled=True)]
    reduce_scatter x1 -> x0, waiting for transfers between devices: 54 us -> none  [per_device(): lax.psum_scatter(jnp.dot(flat_rows, out_weight, preferred_element_type=jn...]
    dot_general x3 -> x0, matrix products: 16.9 us -> none  [the longest x1 13.8 us: per_device(): jnp.dot(flat_rows, out_weight, preferred_element_type=jnp.float32)]
    reduce_sum x3 -> x0, other arithmetic: 3.64 us -> none  [the longest x1 1.97 us: per_device(): jnp.sum(jnp.where(jnp.arange(DOCS, dtype=jnp.int32) == query_doc[0], doc_...]
    another operation x3 -> x0, local copies, waits for them, and re-layouts: 3.25 us -> none  [the longest x1 1.58 us: attend(): value_heads = value_block.reshape(key_count, kv_heads, HEAD_WIDTH)]
  transfers between devices with their start and end apart: 3 -> 0, of which waited for: 2 -> 0; matrix products, arithmetic and copies ran while one was open for 7% -> 0% of each run, Pallas kernels for 0% -> 0%
where the time goes in v1:
time: 99.7 us; the launch traced here: 99.6 us
  Pallas kernels  97.2 us (97%)
  local copies, waits for them, and re-layouts  2.3 us (2%)
    pallas_call x1, Pallas kernels, per_device(): pl.pallas_call(functools.partial(kernel, (seqs, groups, n, reach)), out_s...  97.2 us
    unnamed x1, local copies, waits for them, and re-layouts  2.3 us

profile of v1, /device:TPU:24, one launch (start us, length us, event | category | flops | bytes accessed | tf_op | source)
XLA Modules:
  0.0 99.6 jit_solution(1584767529388138255)
XLA Ops:
  0.0 97.2 %shard_map.55 = bf16[1,256,2048]{2,1,0:T(8,128)(2,1)} custom-call(bf16[1,256,2048]{2,1,0:T(8,128)(2,1)} %q_ref.1, bf16[1,256,256]{2,1,0:T(8,128)(2,1)} %k_ref.1, bf16[1,256,256]{2,1,0:T(8,128)(2,1)} %v_ref.1, s32[1,16]{1,0:T(1,128)} %len_ref.1, bf16[2048,2048]{1,0:T(8,128)(2,1)} %w_hbm.1), custom_call_target="tpu_custom_call" | custom-call | tf_op jit(solution)/shard_map/pallas_call | solution.py:281
  97.3 2.3 %copy.7 = bf16[1,256,2048]{2,1,0:T(8,128)(2,1)} copy(bf16[1,256,2048]{2,1,0:T(8,128)(2,1)} %shard_map.55) | data formatting | bytes 2097152
